TPU v7x, 128 devices: a whole 4x4x4 slice. The times are simulated.
128 devices in a mesh: blk: 64 (over z_lo, x, y, core), grp: 2 (over z_hi).
Axes of the slice: x: 4, y: 4, z: 4 (z_hi: 2, z_lo: 2; z = z_hi * 2 + z_lo), core: 2. Of those that a mesh axis runs over, the one named last changes fastest.
Arguments:
- returns: float32 [512, 32768], P(None, ('blk', 'grp')), may hold values from -200 to 200
Outputs:
- correlation: bfloat16 [32768, 32768], P(('blk', 'grp'))
All inputs are finite; a program needn't handle non-finite values.
Results may differ from a plain program's by a relative error of at most 0.0034.
Values may be sent and summed in bfloat16 or wider, within the bound.
A program may use at most 128 MiB of HBM per device.

v0:
```python
import math
import jax
import jax.numpy as jnp
from jax import lax
from jax.sharding import Mesh
from jax.sharding import PartitionSpec as P

BLK_GRP = ("blk_0", "blk_1", "blk_2", "blk_3", "grp")


def by_axis(array, axes):
    for axis in axes:
        array = lax.psum(array, axis)
    return array


def gram_tile(first, second):
    return lax.dot_general(
        first, second, (((0,), (0,)), ((), ())), preferred_element_type=jnp.float32
    )


def shards(returns):
    bar_count = returns.shape[0]
    series_dev = returns.shape[1]
    devices = lax.axis_size(BLK_GRP)
    my_index = lax.axis_index(BLK_GRP)
    summed = by_axis(jnp.sum(returns, axis=1), BLK_GRP)
    market = summed / (series_dev * devices)
    excess = returns - market[:, None]
    deviation = excess - jnp.mean(excess, axis=0, keepdims=True)
    inverse = lax.rsqrt(jnp.mean(deviation * deviation, axis=0, keepdims=True) + 1e-06) / math.sqrt(
        bar_count
    )
    zscores = (deviation * inverse).astype(jnp.bfloat16)
    piece = lax.all_gather(zscores, BLK_GRP, axis=1, tiled=True)
    products = gram_tile(zscores, piece)
    column_block = jnp.arange(piece.shape[1], dtype=jnp.int32) // series_dev
    return jnp.where(column_block[None, :] >= my_index, products, jnp.float32(0.0)).astype(
        jnp.bfloat16
    )


def solution(mesh):
    split = Mesh(
        mesh.devices.reshape(2, 4, 4, 2, mesh.shape["grp"]),
        ("blk_0", "blk_1", "blk_2", "blk_3", "grp"),
    )
    in_specs = (P(None, BLK_GRP),)
    out_specs = P(BLK_GRP, None)
    return jax.shard_map(
        shards, mesh=split, in_specs=in_specs, out_specs=out_specs, check_vma=False
    )
```

profile of v0, /device:TPU:1, one launch (start us, length us, event | category | flops | bytes accessed | tf_op | source)
XLA Modules:
  0.0 429.9 jit_solution(4869989052520204716)
XLA Ops:
  6.5 0.0 all-gather.2.cloned.1.call-start
  6.5 1.2 reduce_sum.27
  7.7 4.8 %psum.35 = f32[512]{0:T(512)S(1)} all-reduce(f32[512]{0:T(512)S(1)} %reduce_sum.27), channel_id=1, replica_groups=mesh['blk_0'=2,'blk_1'=4,'blk_2'=4,'blk_3'=2,'grp'=2] {'blk_0'}, use_global_device_ids=true, to_apply=%region_1.0 | all-reduce | flops 512 | bytes 4096 | tf_op jit(solution)/shard_map/psum | solution.py:13
  12.5 8.4 %psum.36 = f32[512]{0:T(512)S(1)} all-reduce(f32[512]{0:T(512)S(1)} %psum.35), channel_id=1, replica_groups=mesh['blk_0'=2,'blk_1'=4,'blk_2'=4,'blk_3'=2,'grp'=2] {'blk_1'}, use_global_device_ids=true, to_apply=%region_2.0 | all-reduce | flops 512 | bytes 4096 | tf_op jit(solution)/shard_map/psum | solution.py:13
  20.9 8.7 %psum.37 = f32[512]{0:T(512)S(1)} all-reduce(f32[512]{0:T(512)S(1)} %psum.36), channel_id=1, replica_groups=mesh['blk_0'=2,'blk_1'=4,'blk_2'=4,'blk_3'=2,'grp'=2] {'blk_2'}, use_global_device_ids=true, to_apply=%region_3.0 | all-reduce | flops 512 | bytes 4096 | tf_op jit(solution)/shard_map/psum | solution.py:13
  29.6 7.8 %psum.38 = f32[512]{0:T(512)S(1)} all-reduce(f32[512]{0:T(512)S(1)} %psum.37), channel_id=1, replica_groups=mesh['blk_0'=2,'blk_1'=4,'blk_2'=4,'blk_3'=2,'grp'=2] {'blk_3'}, use_global_device_ids=true, to_apply=%region_4.0 | all-reduce | flops 512 | bytes 4096 | tf_op jit(solution)/shard_map/psum | solution.py:13
  37.4 5.9 %psum.39 = f32[512]{0:T(512)S(1)} all-reduce(f32[512]{0:T(512)S(1)} %psum.38), channel_id=1, replica_groups=mesh['blk_0'=2,'blk_1'=4,'blk_2'=4,'blk_3'=2,'grp'=2] {'grp'}, use_global_device_ids=true, to_apply=%region_5.0 | all-reduce | flops 512 | bytes 4096 | tf_op jit(solution)/shard_map/psum | solution.py:13
  43.3 1.2 subtract_reduce_fusion
  44.5 1.2 multiply_reduce_fusion
  45.7 1.9 multiply_convert_fusion
  47.6 0.0 all-gather.2.cloned.1.call-update
  47.7 354.2 %all-gather.2.cloned.1.call-done = bf16[512,32768]{1,0:T(8,128)(2,1)} async-done(((bf16[512,256]{1,0:T(8,128)(2,1)}), bf16[512,32768]{1,0:T(8,128)(2,1)}) %all-gather.2.cloned.1.call-update) | async-done | bytes 33554448 | tf_op jit(solution)/shard_map/all_gather | solution.py:36
  401.9 21.2 %fusion = bf16[256,32768]{1,0:T(8,128)(2,1)} fusion(bf16[512,256]{1,0:T(8,128)(2,1)} %multiply_convert_fusion, bf16[512,32768]{1,0:T(8,128)(2,1)} %all-gather.2.cloned.1.call-done, pred[32768]{0:T(1024)(128)(4,1)S(1)} %fusion.1), kind=kOutput, calls=%fused_computation.1 | convolution fusion | flops 8606711808 | bytes 50626560 | tf_op jit(solution)/shard_map/dot_general | solution.py:18
  (4 shorter events, 0.1 us)
Async XLA Ops:
  6.5 395.3 %all-gather.2.cloned.1.call-start = ((), (), s32[]{:S(2)}) async-start(), calls=%async_computation | async-start | bytes 33816576 | tf_op jit(solution)/shard_map/all_gather | solution.py:36
Sparse Core Ops, SparseCore 0:
  47.8 354.0 all-gather.1
where the time goes:
time: 430 us
  waiting for transfers between devices  354 us (82%)
  blocking collectives  35.6 us (8%)
  matrix products  21.2 us (5%)
  between operations  13.4 us (3%)
  other arithmetic  5.51 us (1%)
    all_gather x1, waiting for transfers between devices, shards(): piece = lax.all_gather(zscores, BLK_GRP, axis=1, tiled=True)  354 us
    psum x5, blocking collectives, by_axis(): array = lax.psum(array, axis)  35.6 us
    dot_general x1, matrix products, gram_tile(): lax.dot_general(first, second, (((0,), (0,)), ((), ())), preferred_elemen...  21.2 us
  transfers between devices with their start and end apart: 1, of which 1 were waited for; matrix products, arithmetic and copies ran while one was open for 0% of the time, Pallas kernels for 0%

commit v1 on v0

--- a/solution.py
+++ b/solution.py
@@ -33,7 +33,9 @@
         bar_count
     )
     zscores = (deviation * inverse).astype(jnp.bfloat16)
-    piece = lax.all_gather(zscores, BLK_GRP, axis=1, tiled=True)
+    piece = jnp.concatenate(
+        lax.all_to_all(jnp.stack([zscores] * lax.axis_size(BLK_GRP)), BLK_GRP, 0, 0), axis=1
+    )
     products = gram_tile(zscores, piece)
     column_block = jnp.arange(piece.shape[1], dtype=jnp.int32) // series_dev
     return jnp.where(column_block[None, :] >= my_index, products, jnp.float32(0.0)).astype(

time: 430 us -> 608 us (1.41)
  the two profiles are of different devices: /device:TPU:1 before, /device:TPU:5 now
where the time goes in v1:
time: 608 us; the launch traced here: 607 us
  waiting for transfers between devices  530 us (87%)
  blocking collectives  32.6 us (5%)
  matrix products  19.1 us (3%)
  local copies, waits for them, and re-layouts  11.2 us (2%)
  starting transfers between devices  9.11 us (1%)
    all_to_all x1, waiting for transfers between devices, shards(): lax.all_to_all(jnp.stack([zscores] * lax.axis_size(BLK_GRP)), BLK_GRP, 0, 0)  530 us
    psum x5, blocking collectives, by_axis(): array = lax.psum(array, axis)  32.6 us
    dot_general x1, matrix products, gram_tile(): lax.dot_general(first, second, (((0,), (0,)), ((), ())), preferred_elemen...  19.1 us
  transfers between devices with their start and end apart: 1, of which 1 were waited for; matrix products, arithmetic and copies ran while one was open for 0% of the time, Pallas kernels for 0%

profile of v1, /device:TPU:5, one launch (start us, length us, event | category | flops | bytes accessed | tf_op | source)
XLA Modules:
  0.0 607.1 jit_solution(6196766640221029567)
XLA Ops:
  0.0 1.2 reduce_sum.27
  1.2 4.0 psum.35
  5.1 6.3 %psum.36 = f32[512]{0:T(512)S(1)} all-reduce(f32[512]{0:T(512)S(1)} %psum.35), channel_id=1, replica_groups=mesh['blk_0'=2,'blk_1'=4,'blk_2'=4,'blk_3'=2,'grp'=2] {'blk_1'}, use_global_device_ids=true, to_apply=%region_2.0 | all-reduce | flops 512 | bytes 4096 | tf_op jit(solution)/shard_map/psum | solution.py:13
  11.4 8.7 %psum.37 = f32[512]{0:T(512)S(1)} all-reduce(f32[512]{0:T(512)S(1)} %psum.36), channel_id=1, replica_groups=mesh['blk_0'=2,'blk_1'=4,'blk_2'=4,'blk_3'=2,'grp'=2] {'blk_2'}, use_global_device_ids=true, to_apply=%region_3.0 | all-reduce | flops 512 | bytes 4096 | tf_op jit(solution)/shard_map/psum | solution.py:13
  20.1 7.8 %psum.38 = f32[512]{0:T(512)S(1)} all-reduce(f32[512]{0:T(512)S(1)} %psum.37), channel_id=1, replica_groups=mesh['blk_0'=2,'blk_1'=4,'blk_2'=4,'blk_3'=2,'grp'=2] {'blk_3'}, use_global_device_ids=true, to_apply=%region_4.0 | all-reduce | flops 512 | bytes 4096 | tf_op jit(solution)/shard_map/psum | solution.py:13
  27.9 5.9 psum.39
  33.8 1.2 subtract_reduce_fusion
  35.0 1.2 multiply_reduce_fusion
  36.2 1.2 multiply_convert_fusion
  37.4 0.1 copy.2
  37.6 11.1 %stack.2 = bf16[128,512,256]{1,2,0:T(8,128)(2,1)} broadcast(bf16[512,256]{0,1:T(8,128)(2,1)S(1)} %copy.2), dimensions={1,2} | broadcast | bytes 33816576 | tf_op jit(solution)/shard_map/stack | solution.py:37
  48.6 9.1 %all-to-all-start = ((bf16[128,512,256]{1,2,0:T(8,128)(2,1)}), bf16[128,512,256]{1,2,0:T(8,128)(2,1)}, u32[]{:S(2)}, u32[]{:S(2)}) async-start(bf16[128,512,256]{1,2,0:T(8,128)(2,1)} %stack.2), calls=%async_computation | async-start | bytes 67108864 | tf_op jit(solution)/shard_map/all_to_all | solution.py:37
  57.8 530.3 %all-to-all-done = bf16[128,512,256]{1,2,0:T(8,128)(2,1)} async-done(((bf16[128,512,256]{1,2,0:T(8,128)(2,1)}), bf16[128,512,256]{1,2,0:T(8,128)(2,1)}, u32[]{:S(2)}, u32[]{:S(2)}) %all-to-all-start) | async-done | bytes 33554464 | tf_op jit(solution)/shard_map/all_to_all | solution.py:37
  588.0 19.1 %fusion = bf16[256,32768]{1,0:T(8,128)(2,1)} fusion(bf16[512,256]{1,0:T(8,128)(2,1)S(1)} %multiply_convert_fusion, bf16[512,32768]{0,1:T(8,128)(2,1)} %bitcast.1, pred[32768]{0:T(1024)(128)(4,1)S(1)} %fusion.1), kind=kOutput, calls=%fused_computation.1 | convolution fusion | flops 8606711808 | bytes 50626560 | tf_op jit(solution)/shard_map/dot_general | solution.py:18
  (4 shorter events, 0.1 us)
Async XLA Ops:
  48.6 539.4 %all-to-all-start = ((bf16[128,512,256]{1,2,0:T(8,128)(2,1)}), bf16[128,512,256]{1,2,0:T(8,128)(2,1)}, u32[]{:S(2)}, u32[]{:S(2)}) async-start(bf16[128,512,256]{1,2,0:T(8,128)(2,1)} %stack.2), calls=%async_computation | async-start | bytes 67108864 | tf_op jit(solution)/shard_map/all_to_all | solution.py:37
